TPU v7x, 512 devices: a whole 4x4x16 slice. The times are simulated.
512 devices in a mesh: dp: 32 (over y, x, core), tensor: 16 (over z).
Axes of the slice: x: 4, y: 4, z: 16, core: 2. Of those that a mesh axis runs over, the one named last changes fastest.
Arguments:
- tokens: bfloat16 [16384, 8192], P('dp', 'tensor'), may hold values from -6 to 6
- out_grad: bfloat16 [16384, 28672], P('dp', 'tensor'), may hold values from -6 to 6
- galore_basis: bfloat16 [8192, 512], P('tensor'), may hold values from -0.0625 to 0.0625
- first_moment: float32 [512, 28672], P('dp', 'tensor'), may hold values from -4 to 4
- second_moment: float32 [512, 28672], P('dp', 'tensor'), may hold values from 0.05 to 5
- list_lengths: int32 [128], P('dp'), may hold values from 1 to 128, as said below
Outputs:
- new_first: float32 [512, 28672], P('dp', 'tensor')
- new_second: float32 [512, 28672], P('dp', 'tensor')
- weight_step: bfloat16 [8192, 28672], P('dp', 'tensor')
Inputs may be any that keep to these rules, and one draw needn't show every extreme that they name: `list_lengths`: live slots of a list come first in its 128 slots.
All inputs are finite; a program needn't handle non-finite values.
Results may differ from a plain program's by a relative error of at most 0.0051.
Values may be sent and summed in bfloat16 or wider, within the bound.
No kernel may reach another device: no remote copies, remote signals or barrier semaphores. Data moves between devices by JAX's collectives and lax.ppermute only.
A program may use at most 64 MiB of HBM per device.

v0:
```python
import jax
import jax.numpy as jnp
from jax import lax
from jax.sharding import PartitionSpec as P

SLOTS = 128
STEP = 1000
beta_first = 0.9
beta_second = 0.999
epsilon = 1e-08
bf16 = jnp.bfloat16
f32 = jnp.float32


def exchange(tiles, axis, groups=None):
    return lax.all_to_all(
        tiles, axis, split_axis=0, concat_axis=0, tiled=True, axis_index_groups=groups
    )


def copies_to_all(x, axis, peers, groups=None):
    return exchange(jnp.broadcast_to(x, (peers, *x.shape)), axis, groups)


def token_weights(list_lengths):
    slot_index = jnp.arange(SLOTS, dtype=jnp.int32)
    live_slots = slot_index[None, :] < list_lengths[:, None]
    scaled = jnp.where(
        live_slots, 1.0 / list_lengths[:, None].astype(jnp.float32), jnp.float32(0.0)
    )
    return scaled.reshape(-1)


def basis_routes(chips, splits):
    return [
        ((2 * k + b) * splits + s, (2 * s + b) * splits + (k - s) % splits)
        for k in range(chips)
        for b in range(2)
        for s in range(splits)
    ]


def body(tokens, out_grad, galore_basis, first_moment, second_moment, list_lengths):
    replicas = lax.axis_size("dp")
    splits = lax.axis_size("tensor")
    chips = replicas // 2
    replica = lax.axis_index("dp")
    core = replica % 2
    rank = galore_basis.shape[1]
    owned = rank // replicas
    columns = out_grad.shape[1]
    slots = tokens.shape[0]
    same_core = [[2 * i + c for i in range(chips)] for c in range(2)]
    partner = [(i, i ^ 1) for i in range(replicas)]
    block_rows = galore_basis.shape[0] * splits // replicas
    half_block = lax.dynamic_slice_in_dim(galore_basis, core * block_rows, block_rows, 0)
    local_basis = lax.ppermute(half_block, ("dp", "tensor"), basis_routes(chips, splits))
    partial = lax.dot_general(
        galore_basis, tokens, (((0,), (1,)), ((), ())), preferred_element_type=f32
    ).astype(bf16)
    arrived = exchange(partial.reshape(splits, rank // splits, slots), "tensor")
    coordinates = arrived.astype(f32).sum(axis=0)
    weighted = (coordinates * token_weights(list_lengths)[None, :]).astype(bf16)
    weighted = lax.all_gather(weighted, "tensor", axis=0, tiled=True)
    by_owner = weighted.reshape(chips, 2, owned, slots)
    other = lax.dynamic_index_in_dim(by_owner, 1 - core, 1, keepdims=False).reshape(
        rank // 2, slots
    )
    own = lax.dynamic_index_in_dim(by_owner, core, 1, keepdims=False).reshape(rank // 2, slots)
    sent = jnp.dot(other, out_grad, preferred_element_type=f32).astype(bf16)
    received = lax.ppermute(sent, "dp", partner)
    kept = jnp.dot(own, out_grad, preferred_element_type=f32)
    chip_sum = (kept + received.astype(f32)).astype(bf16).reshape(chips, owned, columns)
    gradient = exchange(chip_sum, "dp", same_core).astype(f32).sum(axis=0)
    new_first = beta_first * first_moment + (1.0 - beta_first) * gradient
    new_second = beta_second * second_moment + (1.0 - beta_second) * gradient * gradient
    corrected_first = new_first / (1.0 - beta_first**STEP)
    corrected_second = new_second / (1.0 - beta_second**STEP)
    update = (corrected_first / (jnp.sqrt(corrected_second) + epsilon)).astype(bf16)
    own_rows = copies_to_all(update, "dp", chips, same_core).reshape(rank // 2, columns)
    other_rows = lax.ppermute(own_rows, "dp", partner)
    place = jnp.arange(rank, dtype=jnp.int32)
    side = place // (rank // 2)
    within = place % (rank // 2)
    source = (
        within // owned * (2 * owned)
        + jnp.where(side == 0, core, 1 - core) * owned
        + within % owned
    )
    pick = (place[:, None] == source[None, :]).astype(bf16)
    ordered = jnp.dot(local_basis, pick, preferred_element_type=f32).astype(bf16)
    expanded = jnp.dot(ordered[:, : rank // 2], own_rows, preferred_element_type=f32)
    expanded = expanded + jnp.dot(ordered[:, rank // 2 :], other_rows, preferred_element_type=f32)
    weight_step = (-expanded).astype(bf16)
    return (new_first, new_second, weight_step)


def solution(mesh):
    in_specs = (
        P("dp", "tensor"),
        P("dp", "tensor"),
        P("tensor", None),
        P("dp", "tensor"),
        P("dp", "tensor"),
        P("dp"),
    )
    out_specs = (P("dp", "tensor"), P("dp", "tensor"), P("dp", "tensor"))
    return jax.shard_map(body, mesh=mesh, in_specs=in_specs, out_specs=out_specs, check_vma=False)
```

profile of v0, /device:TPU:62, one launch (start us, length us, event | category | flops | bytes accessed | tf_op | source)
XLA Modules:
  0.0 160.9 jit_solution(582919417251868514)
XLA Ops:
  0.6 0.0 copy-start
  0.6 0.0 copy-start.4
  0.7 2.6 %convolution_convert_fusion.1 = bf16[512,512]{1,0:T(8,128)(2,1)} fusion(bf16[512,512]{1,0:T(8,128)(2,1)} %param.8, bf16[512,512]{1,0:T(8,128)(2,1)} %param.6), kind=kOutput, calls=%fused_computation.6 | convolution fusion | flops 268697600 | bytes 1572864 | tf_op jit(solution)/shard_map/dot_general | solution.py:58
  3.3 15.2 %all-to-all-start = ((bf16[16,32,512]{2,1,0:T(8,128)(2,1)}), bf16[16,32,512]{2,1,0:T(8,128)(2,1)S(1)}, u32[]{:S(2)}, u32[]{:S(2)}) async-start(bf16[16,32,512]{2,1,0:T(8,128)(2,1)} %bitcast), calls=%async_computation | async-start | bytes 1048576 | tf_op jit(solution)/shard_map/all_to_all | solution.py:16
  18.5 0.0 copy-done.4
  18.5 0.1 select_bitcast_fusion
  18.6 28.4 %all-to-all-done = bf16[16,32,512]{2,1,0:T(8,128)(2,1)S(1)} async-done(((bf16[16,32,512]{2,1,0:T(8,128)(2,1)}), bf16[16,32,512]{2,1,0:T(8,128)(2,1)S(1)}, u32[]{:S(2)}, u32[]{:S(2)}) %all-to-all-start) | async-done | bytes 524320 | tf_op jit(solution)/shard_map/all_to_all | solution.py:16
  47.0 0.1 convert_reduce_fusion.1
  47.1 30.8 %all_gather.3 = bf16[512,512]{1,0:T(8,128)(2,1)S(1)} all-gather(bf16[32,512]{1,0:T(8,128)(2,1)S(1)} %multiply_convert_fusion), channel_id=1, replica_groups=mesh['dp'=32,'tensor'=16] {'tensor'}, dimensions={0}, use_global_device_ids=true | all-gather | bytes 557056 | tf_op jit(solution)/shard_map/all_gather | solution.py:64
  77.9 0.0 copy-done
  77.9 0.6 convolution_convert_fusion
  78.5 1.9 %collective-permute-start = (bf16[256,1792]{1,0:T(8,128)(2,1)S(1)}, bf16[256,1792]{1,0:T(8,128)(2,1)S(1)}, u32[]{:S(2)}, u32[]{:S(2)}) collective-permute-start(bf16[256,1792]{1,0:T(8,128)(2,1)S(1)} %convolution_convert_fusion), channel_id=1, source_target_pairs={{0,16},{16,0},{32,48},{48,32},{64,80},{80,64},{96,112},{112,96},{1... | collective-permute-start | bytes 2752520 | tf_op jit(solution)/shard_map/ppermute | solution.py:71
  80.5 2.4 %collective-permute-done = bf16[256,1792]{1,0:T(8,128)(2,1)S(1)} collective-permute-done((bf16[256,1792]{1,0:T(8,128)(2,1)S(1)}, bf16[256,1792]{1,0:T(8,128)(2,1)S(1)}, u32[]{:S(2)}, u32[]{:S(2)}) %collective-permute-start) | collective-permute-done | bytes 917536 | tf_op jit(solution)/shard_map/ppermute | solution.py:71
  82.9 0.6 add_convert_fusion
  83.5 0.0 copy-start.2
  83.6 0.0 copy-start.3
  83.6 19.0 %all_to_all.15 = bf16[16,16,1792]{2,1,0:T(8,128)(2,1)S(1)} all-to-all(bf16[16,16,1792]{2,1,0:T(8,128)(2,1)S(1)} %bitcast.19), channel_id=1, replica_groups={{0,32,64,96,128,160,192,224,256,288,320,352,384,416,448,480},{16,48,80,..., dimensions={0} | all-to-all | bytes 1835008 | tf_op jit(solution)/shard_map/all_to_all | solution.py:16
  102.6 0.1 convert_reduce_fusion
  102.7 0.0 copy-done.2
  102.7 0.0 copy-done.3
  102.7 0.0 copy-start.1
  102.7 0.7 divide_convert_fusion
  103.5 0.1 broadcast_in_dim.32
  103.5 18.3 %all_to_all.16 = bf16[16,16,1792]{2,1,0:T(8,128)(2,1)S(1)} all-to-all(bf16[16,16,1792]{2,1,0:T(8,128)(2,1)S(1)} %broadcast_in_dim.32), channel_id=1, replica_groups={{0,32,64,96,128,160,192,224,256,288,320,352,384,416,448,480},{16,48,80,..., dimensions={0} | all-to-all | bytes 1835008 | tf_op jit(solution)/shard_map/all_to_all | solution.py:16
  121.8 1.9 %collective-permute-start.2 = (bf16[256,1792]{1,0:T(8,128)(2,1)S(1)}, bf16[256,1792]{1,0:T(8,128)(2,1)}, u32[]{:S(2)}, u32[]{:S(2)}) collective-permute-start(bf16[256,1792]{1,0:T(8,128)(2,1)S(1)} %bitcast.17), channel_id=1, source_target_pairs={{0,16},{16,0},{32,48},{48,32},{64,80},{80,64},{96,112},{112,96},{1... | collective-permute-start | bytes 2752520 | tf_op jit(solution)/shard_map/ppermute | solution.py:81
  123.7 0.0 copy-done.1
  123.8 8.3 %collective-permute-start.1 = (bf16[256,512]{1,0:T(8,128)(2,1)S(1)}, bf16[256,512]{1,0:T(8,128)(2,1)S(1)}, u32[]{:S(2)}, u32[]{:S(2)}) collective-permute-start(bf16[256,512]{1,0:T(8,128)(2,1)S(1)} %constant_dynamic-slice_fusion), channel_id=1, source_target_pairs={{0,0},{1,47},{2,78},{3,109},{4,140},{5,171},{6,202},{7,233},{8,264... | collective-permute-start | bytes 786440 | tf_op jit(solution)/shard_map/ppermute | solution.py:57
  132.1 25.5 %collective-permute-done.1 = bf16[256,512]{1,0:T(8,128)(2,1)S(1)} collective-permute-done((bf16[256,512]{1,0:T(8,128)(2,1)S(1)}, bf16[256,512]{1,0:T(8,128)(2,1)S(1)}, u32[]{:S(2)}, u32[]{:S(2)}) %collective-permute-start.1) | collective-permute-done | bytes 262176 | tf_op jit(solution)/shard_map/ppermute | solution.py:57
  157.6 0.4 convolution_convert_fusion.2
  157.9 0.4 fusion.4
  158.4 0.0 collective-permute-done.2
  158.4 2.5 %fusion.1 = bf16[256,1792]{1,0:T(8,128)(2,1)} fusion(f32[256,1792]{1,0:T(8,128)S(1)} %fusion.4, bf16[256,1792]{1,0:T(8,128)(2,1)} %collective-permute-done.2, bf16[256,512]{1,0:T(8,128)(2,1)S(1)} %convolution_convert_fusion.2), kind=kOutput, calls=%fused_computation.3 | convolution fusion | flops 236257280 | bytes 3801088 | tf_op jit(solution)/shard_map/dot_general | solution.py:93
  (5 shorter events, 0.1 us)
Async XLA Ops:
  0.6 77.2 %copy-start = (bf16[512,1792]{1,0:T(8,128)(2,1)S(1)}, bf16[512,1792]{1,0:T(8,128)(2,1)}, u32[]{:S(2)}) copy-start(bf16[512,1792]{1,0:T(8,128)(2,1)} %param.7) | copy-start | bytes 5505028
  0.6 17.8 %copy-start.4 = (s32[4]{0:T(128)S(1)}, s32[4]{0:T(128)}, u32[]{:S(2)}) copy-start(s32[4]{0:T(128)} %param.11) | copy-start | bytes 52
  3.3 43.7 %all-to-all-start = ((bf16[16,32,512]{2,1,0:T(8,128)(2,1)}), bf16[16,32,512]{2,1,0:T(8,128)(2,1)S(1)}, u32[]{:S(2)}, u32[]{:S(2)}) async-start(bf16[16,32,512]{2,1,0:T(8,128)(2,1)} %bitcast), calls=%async_computation | async-start | bytes 1048576 | tf_op jit(solution)/shard_map/all_to_all | solution.py:16
  78.5 4.4 %collective-permute-start = (bf16[256,1792]{1,0:T(8,128)(2,1)S(1)}, bf16[256,1792]{1,0:T(8,128)(2,1)S(1)}, u32[]{:S(2)}, u32[]{:S(2)}) collective-permute-start(bf16[256,1792]{1,0:T(8,128)(2,1)S(1)} %convolution_convert_fusion), channel_id=1, source_target_pairs={{0,16},{16,0},{32,48},{48,32},{64,80},{80,64},{96,112},{112,96},{1... | collective-permute-start | bytes 2752520 | tf_op jit(solution)/shard_map/ppermute | solution.py:71
  83.5 19.2 %copy-start.2 = (f32[16,1792]{1,0:T(8,128)S(1)}, f32[16,1792]{1,0:T(8,128)}, u32[]{:S(2)}) copy-start(f32[16,1792]{1,0:T(8,128)} %param.10) | copy-start | bytes 344068
  83.6 19.1 %copy-start.3 = (f32[16,1792]{1,0:T(8,128)S(1)}, f32[16,1792]{1,0:T(8,128)}, u32[]{:S(2)}) copy-start(f32[16,1792]{1,0:T(8,128)} %param.9) | copy-start | bytes 344068
  102.7 21.0 %copy-start.1 = (bf16[512,512]{1,0:T(8,128)(2,1)S(1)}, bf16[512,512]{1,0:T(8,128)(2,1)}, u32[]{:S(2)}) copy-start(bf16[512,512]{1,0:T(8,128)(2,1)} %param.8) | copy-start | bytes 1572868
  121.8 36.6 %collective-permute-start.2 = (bf16[256,1792]{1,0:T(8,128)(2,1)S(1)}, bf16[256,1792]{1,0:T(8,128)(2,1)}, u32[]{:S(2)}, u32[]{:S(2)}) collective-permute-start(bf16[256,1792]{1,0:T(8,128)(2,1)S(1)} %bitcast.17), channel_id=1, source_target_pairs={{0,16},{16,0},{32,48},{48,32},{64,80},{80,64},{96,112},{112,96},{1... | collective-permute-start | bytes 2752520 | tf_op jit(solution)/shard_map/ppermute | solution.py:81
  123.8 33.8 %collective-permute-start.1 = (bf16[256,512]{1,0:T(8,128)(2,1)S(1)}, bf16[256,512]{1,0:T(8,128)(2,1)S(1)}, u32[]{:S(2)}, u32[]{:S(2)}) collective-permute-start(bf16[256,512]{1,0:T(8,128)(2,1)S(1)} %constant_dynamic-slice_fusion), channel_id=1, source_target_pairs={{0,0},{1,47},{2,78},{3,109},{4,140},{5,171},{6,202},{7,233},{8,264... | collective-permute-start | bytes 786440 | tf_op jit(solution)/shard_map/ppermute | solution.py:57
where the time goes:
time: 161 us
  blocking collectives  68 us (42%)
  waiting for transfers between devices  56.3 us (35%)
  starting transfers between devices  27.3 us (17%)
  matrix products  7.21 us (4%)
    all_to_all x2, blocking collectives, exchange(): lax.all_to_all(tiles, axis, split_axis=0, concat_axis=0, tiled=True, axis...  37.3 us
    all_gather x1, blocking collectives, body(): weighted = lax.all_gather(weighted, 'tensor', axis=0, tiled=True)  30.8 us
    all_to_all x1, waiting for transfers between devices, exchange(): lax.all_to_all(tiles, axis, split_axis=0, concat_axis=0, tiled=True, axis...  28.4 us
    ppermute x1, waiting for transfers between devices, body(): lax.ppermute(half_block, ('dp', 'tensor'), basis_routes(chips, splits))  25.5 us
    all_to_all x1, starting transfers between devices, exchange(): lax.all_to_all(tiles, axis, split_axis=0, concat_axis=0, tiled=True, axis...  15.2 us
    ppermute x1, starting transfers between devices, body(): lax.ppermute(half_block, ('dp', 'tensor'), basis_routes(chips, splits))  8.29 us
  transfers between devices with their start and end apart: 4, of which 3 were waited for; matrix products, arithmetic and copies ran while one was open for 1% of the time, Pallas kernels for 0%

commit v1 on v0

--- a/solution.py
+++ b/solution.py
@@ -10,6 +10,13 @@
 epsilon = 1e-08
 bf16 = jnp.bfloat16
 f32 = jnp.float32
+
+
+def edit_zones_over_axis(field_in, in_dim):
+    field_in = jnp.moveaxis(field_in, 0, in_dim)
+    v1 = field_in.shape
+    carry_in = field_in.reshape(*v1[:in_dim], v1[in_dim] * v1[in_dim + 1], *v1[in_dim + 2 :])
+    return carry_in
 
 
 def exchange(tiles, axis, groups=None):
@@ -61,7 +68,21 @@
     arrived = exchange(partial.reshape(splits, rank // splits, slots), "tensor")
     coordinates = arrived.astype(f32).sum(axis=0)
     weighted = (coordinates * token_weights(list_lengths)[None, :]).astype(bf16)
-    weighted = lax.all_gather(weighted, "tensor", axis=0, tiled=True)
+    dev_n = lax.axis_size("tensor")
+    all_blocks = [(to_i, (to_i + 1) % dev_n) for to_i in range(dev_n)]
+    found_now, y2 = ([], [])
+    row_list = [(q, d) for d, q in all_blocks]
+    for pp in range(dev_n - 1):
+        if pp % 2 == 0:
+            found_now.append(
+                lax.ppermute(found_now[-1] if found_now else weighted, "tensor", all_blocks)
+            )
+        else:
+            y2.append(lax.ppermute(y2[-1] if y2 else weighted, "tensor", row_list))
+    ready = jnp.stack([*found_now[::-1], weighted, *y2])
+    work_now = lax.axis_index("tensor") - len(found_now)
+    ready = ready[(jnp.arange(dev_n) - work_now) % dev_n]
+    weighted = edit_zones_over_axis(ready, 0)
     by_owner = weighted.reshape(chips, 2, owned, slots)
     other = lax.dynamic_index_in_dim(by_owner, 1 - core, 1, keepdims=False).reshape(
         rank // 2, slots

time: 161 us -> 191 us (1.19)
  starting transfers between devices: 27.3 us -> 80.6 us
  blocking collectives: 68 us -> 37.2 us
  waiting for transfers between devices: 56.3 us -> 61.6 us
    ppermute x0 -> x15, starting transfers between devices: none -> 51.6 us  [the longest x7 35.5 us: body(): y2.append(lax.ppermute(y2[-1] if y2 else weighted, 'tensor', row_list))]
    all_gather x1 -> x0, blocking collectives: 30.8 us -> none  [body(): weighted = lax.all_gather(weighted, 'tensor', axis=0, tiled=True)]
    ppermute x0 -> x15, waiting for transfers between devices: none -> 5.16 us  [the longest x8 3.77 us: body(): lax.ppermute(found_now[-1] if found_now else weighted, 'tensor', all_blocks)]
  transfers between devices with their start and end apart: 4 -> 19, of which waited for: 3 -> 5; matrix products, arithmetic and copies ran while one was open for 1% -> 1% of each run, Pallas kernels for 0% -> 0%
where the time goes in v1:
time: 191 us; the launch traced here: 190 us
  starting transfers between devices  80.6 us (42%)
  waiting for transfers between devices  61.6 us (32%)
  blocking collectives  37.2 us (19%)
  matrix products  7.21 us (4%)
    all_to_all x2, blocking collectives, exchange(): lax.all_to_all(tiles, axis, split_axis=0, concat_axis=0, tiled=True, axis...  37.2 us
    ppermute x7, starting transfers between devices, body(): y2.append(lax.ppermute(y2[-1] if y2 else weighted, 'tensor', row_list))  35.5 us
    all_to_all x1, waiting for transfers between devices, exchange(): lax.all_to_all(tiles, axis, split_axis=0, concat_axis=0, tiled=True, axis...  28.4 us
    ppermute x1, waiting for transfers between devices, body(): lax.ppermute(half_block, ('dp', 'tensor'), basis_routes(chips, splits))  25.5 us
    ppermute x8, starting transfers between devices, body(): lax.ppermute(found_now[-1] if found_now else weighted, 'tensor', all_blocks)  16 us
    all_to_all x1, starting transfers between devices, exchange(): lax.all_to_all(tiles, axis, split_axis=0, concat_axis=0, tiled=True, axis...  15.2 us
    ppermute x1, starting transfers between devices, body(): lax.ppermute(half_block, ('dp', 'tensor'), basis_routes(chips, splits))  9.95 us
  transfers between devices with their start and end apart: 19, of which 5 were waited for; matrix products, arithmetic and copies ran while one was open for 1% of the time, Pallas kernels for 0%

profile of v1, /device:TPU:62, one launch (start us, length us, event | category | flops | bytes accessed | tf_op | source)
XLA Modules:
  0.0 189.6 jit_solution(13228799988692870)
XLA Ops:
  0.6 0.0 copy-start
  0.6 0.0 copy-start.4
  0.7 2.6 %convolution_convert_fusion.1 = bf16[512,512]{1,0:T(8,128)(2,1)} fusion(bf16[512,512]{1,0:T(8,128)(2,1)} %param.8, bf16[512,512]{1,0:T(8,128)(2,1)} %param.6), kind=kOutput, calls=%fused_computation.7 | convolution fusion | flops 268697600 | bytes 1572864 | tf_op jit(solution)/shard_map/dot_general | solution.py:65
  3.3 15.2 %all-to-all-start = ((bf16[16,32,512]{2,1,0:T(8,128)(2,1)}), bf16[16,32,512]{2,1,0:T(8,128)(2,1)S(1)}, u32[]{:S(2)}, u32[]{:S(2)}) async-start(bf16[16,32,512]{2,1,0:T(8,128)(2,1)} %bitcast), calls=%async_computation | async-start | bytes 1048576 | tf_op jit(solution)/shard_map/all_to_all | solution.py:23
  18.5 0.0 copy-done.4
  18.5 0.1 select_bitcast_fusion
  18.6 28.4 %all-to-all-done = bf16[16,32,512]{2,1,0:T(8,128)(2,1)S(1)} async-done(((bf16[16,32,512]{2,1,0:T(8,128)(2,1)}), bf16[16,32,512]{2,1,0:T(8,128)(2,1)S(1)}, u32[]{:S(2)}, u32[]{:S(2)}) %all-to-all-start) | async-done | bytes 524320 | tf_op jit(solution)/shard_map/all_to_all | solution.py:23
  47.0 0.1 convert_reduce_fusion.1
  47.1 2.1 %collective-permute-start = (bf16[32,512]{1,0:T(8,128)(2,1)S(1)}, bf16[32,512]{1,0:T(8,128)(2,1)S(1)}, u32[]{:S(2)}, u32[]{:S(2)}) collective-permute-start(bf16[32,512]{1,0:T(8,128)(2,1)S(1)} %multiply_convert_fusion), channel_id=1, source_target_pairs={{0,1},{1,2},{2,3},{3,4},{4,5},{5,6},{6,7},{7,8},{8,9},{9,10},{10,1... | collective-permute-start | bytes 98312 | tf_op jit(solution)/shard_map/ppermute | solution.py:78
  49.2 3.8 %collective-permute-done = bf16[32,512]{1,0:T(8,128)(2,1)S(1)} collective-permute-done((bf16[32,512]{1,0:T(8,128)(2,1)S(1)}, bf16[32,512]{1,0:T(8,128)(2,1)S(1)}, u32[]{:S(2)}, u32[]{:S(2)}) %collective-permute-start) | collective-permute-done | bytes 32800 | tf_op jit(solution)/shard_map/ppermute | solution.py:78
  52.9 2.4 %collective-permute-start.1 = (bf16[32,512]{1,0:T(8,128)(2,1)S(1)}, bf16[32,512]{1,0:T(8,128)(2,1)S(1)}, u32[]{:S(2)}, u32[]{:S(2)}) collective-permute-start(bf16[32,512]{1,0:T(8,128)(2,1)S(1)} %collective-permute-done), channel_id=1, source_target_pairs={{0,1},{1,2},{2,3},{3,4},{4,5},{5,6},{6,7},{7,8},{8,9},{9,10},{10,1... | collective-permute-start | bytes 98312 | tf_op jit(solution)/shard_map/ppermute | solution.py:78
  55.3 4.7 %collective-permute-start.8 = (bf16[32,512]{1,0:T(8,128)(2,1)S(1)}, bf16[32,512]{1,0:T(8,128)(2,1)S(1)}, u32[]{:S(2)}, u32[]{:S(2)}) collective-permute-start(bf16[32,512]{1,0:T(8,128)(2,1)S(1)} %multiply_convert_fusion), channel_id=1, source_target_pairs={{1,0},{2,1},{3,2},{4,3},{5,4},{6,5},{7,6},{8,7},{9,8},{10,9},{11,1... | collective-permute-start | bytes 98312 | tf_op jit(solution)/shard_map/ppermute | solution.py:81
  60.1 0.0 collective-permute-done.1
  60.1 1.9 %collective-permute-start.2 = (bf16[32,512]{1,0:T(8,128)(2,1)S(1)}, bf16[32,512]{1,0:T(8,128)(2,1)S(1)}, u32[]{:S(2)}, u32[]{:S(2)}) collective-permute-start(bf16[32,512]{1,0:T(8,128)(2,1)S(1)} %collective-permute-done.1), channel_id=1, source_target_pairs={{0,1},{1,2},{2,3},{3,4},{4,5},{5,6},{6,7},{7,8},{8,9},{9,10},{10,1... | collective-permute-start | bytes 98312 | tf_op jit(solution)/shard_map/ppermute | solution.py:78
  62.0 0.0 collective-permute-done.8
  62.0 5.1 %collective-permute-start.9 = (bf16[32,512]{1,0:T(8,128)(2,1)S(1)}, bf16[32,512]{1,0:T(8,128)(2,1)S(1)}, u32[]{:S(2)}, u32[]{:S(2)}) collective-permute-start(bf16[32,512]{1,0:T(8,128)(2,1)S(1)} %collective-permute-done.8), channel_id=1, source_target_pairs={{1,0},{2,1},{3,2},{4,3},{5,4},{6,5},{7,6},{8,7},{9,8},{10,9},{11,1... | collective-permute-start | bytes 98312 | tf_op jit(solution)/shard_map/ppermute | solution.py:81
  67.2 0.0 collective-permute-done.2
  67.2 1.9 %collective-permute-start.3 = (bf16[32,512]{1,0:T(8,128)(2,1)S(1)}, bf16[32,512]{1,0:T(8,128)(2,1)S(1)}, u32[]{:S(2)}, u32[]{:S(2)}) collective-permute-start(bf16[32,512]{1,0:T(8,128)(2,1)S(1)} %collective-permute-done.2), channel_id=1, source_target_pairs={{0,1},{1,2},{2,3},{3,4},{4,5},{5,6},{6,7},{7,8},{8,9},{9,10},{10,1... | collective-permute-start | bytes 98312 | tf_op jit(solution)/shard_map/ppermute | solution.py:78
  69.1 0.0 collective-permute-done.9
  69.1 5.1 %collective-permute-start.10 = (bf16[32,512]{1,0:T(8,128)(2,1)S(1)}, bf16[32,512]{1,0:T(8,128)(2,1)S(1)}, u32[]{:S(2)}, u32[]{:S(2)}) collective-permute-start(bf16[32,512]{1,0:T(8,128)(2,1)S(1)} %collective-permute-done.9), channel_id=1, source_target_pairs={{1,0},{2,1},{3,2},{4,3},{5,4},{6,5},{7,6},{8,7},{9,8},{10,9},{11,1... | collective-permute-start | bytes 98312 | tf_op jit(solution)/shard_map/ppermute | solution.py:81
  74.3 0.0 collective-permute-done.3
  74.3 1.9 %collective-permute-start.4 = (bf16[32,512]{1,0:T(8,128)(2,1)S(1)}, bf16[32,512]{1,0:T(8,128)(2,1)S(1)}, u32[]{:S(2)}, u32[]{:S(2)}) collective-permute-start(bf16[32,512]{1,0:T(8,128)(2,1)S(1)} %collective-permute-done.3), channel_id=1, source_target_pairs={{0,1},{1,2},{2,3},{3,4},{4,5},{5,6},{6,7},{7,8},{8,9},{9,10},{10,1... | collective-permute-start | bytes 98312 | tf_op jit(solution)/shard_map/ppermute | solution.py:78
  76.2 0.0 collective-permute-done.10
  76.2 5.1 %collective-permute-start.11 = (bf16[32,512]{1,0:T(8,128)(2,1)S(1)}, bf16[32,512]{1,0:T(8,128)(2,1)S(1)}, u32[]{:S(2)}, u32[]{:S(2)}) collective-permute-start(bf16[32,512]{1,0:T(8,128)(2,1)S(1)} %collective-permute-done.10), channel_id=1, source_target_pairs={{1,0},{2,1},{3,2},{4,3},{5,4},{6,5},{7,6},{8,7},{9,8},{10,9},{11,1... | collective-permute-start | bytes 98312 | tf_op jit(solution)/shard_map/ppermute | solution.py:81
  81.4 0.0 collective-permute-done.4
  81.4 1.9 %collective-permute-start.5 = (bf16[32,512]{1,0:T(8,128)(2,1)S(1)}, bf16[32,512]{1,0:T(8,128)(2,1)S(1)}, u32[]{:S(2)}, u32[]{:S(2)}) collective-permute-start(bf16[32,512]{1,0:T(8,128)(2,1)S(1)} %collective-permute-done.4), channel_id=1, source_target_pairs={{0,1},{1,2},{2,3},{3,4},{4,5},{5,6},{6,7},{7,8},{8,9},{9,10},{10,1... | collective-permute-start | bytes 98312 | tf_op jit(solution)/shard_map/ppermute | solution.py:78
  83.3 0.0 collective-permute-done.11
  83.3 5.1 %collective-permute-start.12 = (bf16[32,512]{1,0:T(8,128)(2,1)S(1)}, bf16[32,512]{1,0:T(8,128)(2,1)S(1)}, u32[]{:S(2)}, u32[]{:S(2)}) collective-permute-start(bf16[32,512]{1,0:T(8,128)(2,1)S(1)} %collective-permute-done.11), channel_id=1, source_target_pairs={{1,0},{2,1},{3,2},{4,3},{5,4},{6,5},{7,6},{8,7},{9,8},{10,9},{11,1... | collective-permute-start | bytes 98312 | tf_op jit(solution)/shard_map/ppermute | solution.py:81
  88.5 0.0 collective-permute-done.5
  88.5 1.9 %collective-permute-start.6 = (bf16[32,512]{1,0:T(8,128)(2,1)S(1)}, bf16[32,512]{1,0:T(8,128)(2,1)S(1)}, u32[]{:S(2)}, u32[]{:S(2)}) collective-permute-start(bf16[32,512]{1,0:T(8,128)(2,1)S(1)} %collective-permute-done.5), channel_id=1, source_target_pairs={{0,1},{1,2},{2,3},{3,4},{4,5},{5,6},{6,7},{7,8},{8,9},{9,10},{10,1... | collective-permute-start | bytes 98312 | tf_op jit(solution)/shard_map/ppermute | solution.py:78
  90.4 0.0 collective-permute-done.12
  90.4 5.1 %collective-permute-start.13 = (bf16[32,512]{1,0:T(8,128)(2,1)S(1)}, bf16[32,512]{1,0:T(8,128)(2,1)S(1)}, u32[]{:S(2)}, u32[]{:S(2)}) collective-permute-start(bf16[32,512]{1,0:T(8,128)(2,1)S(1)} %collective-permute-done.12), channel_id=1, source_target_pairs={{1,0},{2,1},{3,2},{4,3},{5,4},{6,5},{7,6},{8,7},{9,8},{10,9},{11,1... | collective-permute-start | bytes 98312 | tf_op jit(solution)/shard_map/ppermute | solution.py:81
  95.6 0.0 collective-permute-done.6
  95.6 1.9 %collective-permute-start.7 = (bf16[32,512]{1,0:T(8,128)(2,1)S(1)}, bf16[32,512]{1,0:T(8,128)(2,1)S(1)}, u32[]{:S(2)}, u32[]{:S(2)}) collective-permute-start(bf16[32,512]{1,0:T(8,128)(2,1)S(1)} %collective-permute-done.6), channel_id=1, source_target_pairs={{0,1},{1,2},{2,3},{3,4},{4,5},{5,6},{6,7},{7,8},{8,9},{9,10},{10,1... | collective-permute-start | bytes 98312 | tf_op jit(solution)/shard_map/ppermute | solution.py:78
  97.5 0.0 collective-permute-done.13
  97.6 5.1 %collective-permute-start.14 = (bf16[32,512]{1,0:T(8,128)(2,1)S(1)}, bf16[32,512]{1,0:T(8,128)(2,1)S(1)}, u32[]{:S(2)}, u32[]{:S(2)}) collective-permute-start(bf16[32,512]{1,0:T(8,128)(2,1)S(1)} %collective-permute-done.13), channel_id=1, source_target_pairs={{1,0},{2,1},{3,2},{4,3},{5,4},{6,5},{7,6},{8,7},{9,8},{10,9},{11,1... | collective-permute-start | bytes 98312 | tf_op jit(solution)/shard_map/ppermute | solution.py:81
  102.7 0.0 collective-permute-done.7
  102.9 1.4 collective-permute-done.14
  104.3 0.6 gather_fusion
  104.9 0.0 copy-done
  104.9 0.6 convolution_convert_fusion
  105.6 1.9 %collective-permute-start.15 = (bf16[256,1792]{1,0:T(8,128)(2,1)S(1)}, bf16[256,1792]{1,0:T(8,128)(2,1)S(1)}, u32[]{:S(2)}, u32[]{:S(2)}) collective-permute-start(bf16[256,1792]{1,0:T(8,128)(2,1)S(1)} %convolution_convert_fusion), channel_id=1, source_target_pairs={{0,16},{16,0},{32,48},{48,32},{64,80},{80,64},{96,112},{112,96},{1... | collective-permute-start | bytes 2752520 | tf_op jit(solution)/shard_map/ppermute | solution.py:92
  107.5 2.4 %collective-permute-done.15 = bf16[256,1792]{1,0:T(8,128)(2,1)S(1)} collective-permute-done((bf16[256,1792]{1,0:T(8,128)(2,1)S(1)}, bf16[256,1792]{1,0:T(8,128)(2,1)S(1)}, u32[]{:S(2)}, u32[]{:S(2)}) %collective-permute-start.15) | collective-permute-done | bytes 917536 | tf_op jit(solution)/shard_map/ppermute | solution.py:92
  109.9 0.6 add_convert_fusion
  110.6 0.0 copy-start.2
  110.6 0.0 copy-start.3
  110.6 19.0 %all_to_all.15 = bf16[16,16,1792]{2,1,0:T(8,128)(2,1)S(1)} all-to-all(bf16[16,16,1792]{2,1,0:T(8,128)(2,1)S(1)} %bitcast.57), channel_id=1, replica_groups={{0,32,64,96,128,160,192,224,256,288,320,352,384,416,448,480},{16,48,80,..., dimensions={0} | all-to-all | bytes 1835008 | tf_op jit(solution)/shard_map/all_to_all | solution.py:23
  129.6 0.1 convert_reduce_fusion
  129.7 0.0 copy-done.2
  129.7 0.0 copy-done.3
  129.7 0.0 copy-start.1
  129.8 0.7 divide_convert_fusion
  130.5 0.1 broadcast_in_dim.33
  130.6 18.3 %all_to_all.16 = bf16[16,16,1792]{2,1,0:T(8,128)(2,1)S(1)} all-to-all(bf16[16,16,1792]{2,1,0:T(8,128)(2,1)S(1)} %broadcast_in_dim.33), channel_id=1, replica_groups={{0,32,64,96,128,160,192,224,256,288,320,352,384,416,448,480},{16,48,80,..., dimensions={0} | all-to-all | bytes 1835008 | tf_op jit(solution)/shard_map/all_to_all | solution.py:23
  148.8 1.9 %collective-permute-start.17 = (bf16[256,1792]{1,0:T(8,128)(2,1)S(1)}, bf16[256,1792]{1,0:T(8,128)(2,1)}, u32[]{:S(2)}, u32[]{:S(2)}) collective-permute-start(bf16[256,1792]{1,0:T(8,128)(2,1)S(1)} %bitcast.55), channel_id=1, source_target_pairs={{0,16},{16,0},{32,48},{48,32},{64,80},{80,64},{96,112},{112,96},{1... | collective-permute-start | bytes 2752520 | tf_op jit(solution)/shard_map/ppermute | solution.py:102
  150.8 0.0 copy-done.1
  150.8 9.9 %collective-permute-start.16 = (bf16[256,512]{1,0:T(8,128)(2,1)S(1)}, bf16[256,512]{1,0:T(8,128)(2,1)S(1)}, u32[]{:S(2)}, u32[]{:S(2)}) collective-permute-start(bf16[256,512]{1,0:T(8,128)(2,1)S(1)} %constant_dynamic-slice_fusion), channel_id=1, source_target_pairs={{0,0},{1,47},{2,78},{3,109},{4,140},{5,171},{6,202},{7,233},{8,264... | collective-permute-start | bytes 786440 | tf_op jit(solution)/shard_map/ppermute | solution.py:64
  160.8 25.5 %collective-permute-done.16 = bf16[256,512]{1,0:T(8,128)(2,1)S(1)} collective-permute-done((bf16[256,512]{1,0:T(8,128)(2,1)S(1)}, bf16[256,512]{1,0:T(8,128)(2,1)S(1)}, u32[]{:S(2)}, u32[]{:S(2)}) %collective-permute-start.16) | collective-permute-done | bytes 262176 | tf_op jit(solution)/shard_map/ppermute | solution.py:64
  186.3 0.4 convolution_convert_fusion.2
  186.7 0.4 fusion.4
  187.1 0.0 collective-permute-done.17
  187.1 2.5 %fusion.1 = bf16[256,1792]{1,0:T(8,128)(2,1)} fusion(f32[256,1792]{1,0:T(8,128)S(1)} %fusion.4, bf16[256,1792]{1,0:T(8,128)(2,1)} %collective-permute-done.17, bf16[256,512]{1,0:T(8,128)(2,1)S(1)} %convolution_convert_fusion.2), kind=kOutput, calls=%fused_computation.4 | convolution fusion | flops 236257280 | bytes 3801088 | tf_op jit(solution)/shard_map/dot_general | solution.py:114
  (23 shorter events, 0.2 us)
Async XLA Ops:
  0.6 104.3 %copy-start = (bf16[512,1792]{1,0:T(8,128)(2,1)S(1)}, bf16[512,1792]{1,0:T(8,128)(2,1)}, u32[]{:S(2)}) copy-start(bf16[512,1792]{1,0:T(8,128)(2,1)} %param.7) | copy-start | bytes 5505028
  0.6 17.8 %copy-start.4 = (s32[4]{0:T(128)S(1)}, s32[4]{0:T(128)}, u32[]{:S(2)}) copy-start(s32[4]{0:T(128)} %param.11) | copy-start | bytes 52
  3.3 43.7 %all-to-all-start = ((bf16[16,32,512]{2,1,0:T(8,128)(2,1)}), bf16[16,32,512]{2,1,0:T(8,128)(2,1)S(1)}, u32[]{:S(2)}, u32[]{:S(2)}) async-start(bf16[16,32,512]{2,1,0:T(8,128)(2,1)} %bitcast), calls=%async_computation | async-start | bytes 1048576 | tf_op jit(solution)/shard_map/all_to_all | solution.py:23
  47.1 5.8 %collective-permute-start = (bf16[32,512]{1,0:T(8,128)(2,1)S(1)}, bf16[32,512]{1,0:T(8,128)(2,1)S(1)}, u32[]{:S(2)}, u32[]{:S(2)}) collective-permute-start(bf16[32,512]{1,0:T(8,128)(2,1)S(1)} %multiply_convert_fusion), channel_id=1, source_target_pairs={{0,1},{1,2},{2,3},{3,4},{4,5},{5,6},{6,7},{7,8},{8,9},{9,10},{10,1... | collective-permute-start | bytes 98312 | tf_op jit(solution)/shard_map/ppermute | solution.py:78
  52.9 7.2 %collective-permute-start.1 = (bf16[32,512]{1,0:T(8,128)(2,1)S(1)}, bf16[32,512]{1,0:T(8,128)(2,1)S(1)}, u32[]{:S(2)}, u32[]{:S(2)}) collective-permute-start(bf16[32,512]{1,0:T(8,128)(2,1)S(1)} %collective-permute-done), channel_id=1, source_target_pairs={{0,1},{1,2},{2,3},{3,4},{4,5},{5,6},{6,7},{7,8},{8,9},{9,10},{10,1... | collective-permute-start | bytes 98312 | tf_op jit(solution)/shard_map/ppermute | solution.py:78
  55.3 6.7 %collective-permute-start.8 = (bf16[32,512]{1,0:T(8,128)(2,1)S(1)}, bf16[32,512]{1,0:T(8,128)(2,1)S(1)}, u32[]{:S(2)}, u32[]{:S(2)}) collective-permute-start(bf16[32,512]{1,0:T(8,128)(2,1)S(1)} %multiply_convert_fusion), channel_id=1, source_target_pairs={{1,0},{2,1},{3,2},{4,3},{5,4},{6,5},{7,6},{8,7},{9,8},{10,9},{11,1... | collective-permute-start | bytes 98312 | tf_op jit(solution)/shard_map/ppermute | solution.py:81
  60.1 7.1 %collective-permute-start.2 = (bf16[32,512]{1,0:T(8,128)(2,1)S(1)}, bf16[32,512]{1,0:T(8,128)(2,1)S(1)}, u32[]{:S(2)}, u32[]{:S(2)}) collective-permute-start(bf16[32,512]{1,0:T(8,128)(2,1)S(1)} %collective-permute-done.1), channel_id=1, source_target_pairs={{0,1},{1,2},{2,3},{3,4},{4,5},{5,6},{6,7},{7,8},{8,9},{9,10},{10,1... | collective-permute-start | bytes 98312 | tf_op jit(solution)/shard_map/ppermute | solution.py:78
  62.0 7.1 %collective-permute-start.9 = (bf16[32,512]{1,0:T(8,128)(2,1)S(1)}, bf16[32,512]{1,0:T(8,128)(2,1)S(1)}, u32[]{:S(2)}, u32[]{:S(2)}) collective-permute-start(bf16[32,512]{1,0:T(8,128)(2,1)S(1)} %collective-permute-done.8), channel_id=1, source_target_pairs={{1,0},{2,1},{3,2},{4,3},{5,4},{6,5},{7,6},{8,7},{9,8},{10,9},{11,1... | collective-permute-start | bytes 98312 | tf_op jit(solution)/shard_map/ppermute | solution.py:81
  67.2 7.1 %collective-permute-start.3 = (bf16[32,512]{1,0:T(8,128)(2,1)S(1)}, bf16[32,512]{1,0:T(8,128)(2,1)S(1)}, u32[]{:S(2)}, u32[]{:S(2)}) collective-permute-start(bf16[32,512]{1,0:T(8,128)(2,1)S(1)} %collective-permute-done.2), channel_id=1, source_target_pairs={{0,1},{1,2},{2,3},{3,4},{4,5},{5,6},{6,7},{7,8},{8,9},{9,10},{10,1... | collective-permute-start | bytes 98312 | tf_op jit(solution)/shard_map/ppermute | solution.py:78
  69.1 7.1 %collective-permute-start.10 = (bf16[32,512]{1,0:T(8,128)(2,1)S(1)}, bf16[32,512]{1,0:T(8,128)(2,1)S(1)}, u32[]{:S(2)}, u32[]{:S(2)}) collective-permute-start(bf16[32,512]{1,0:T(8,128)(2,1)S(1)} %collective-permute-done.9), channel_id=1, source_target_pairs={{1,0},{2,1},{3,2},{4,3},{5,4},{6,5},{7,6},{8,7},{9,8},{10,9},{11,1... | collective-permute-start | bytes 98312 | tf_op jit(solution)/shard_map/ppermute | solution.py:81
  74.3 7.1 %collective-permute-start.4 = (bf16[32,512]{1,0:T(8,128)(2,1)S(1)}, bf16[32,512]{1,0:T(8,128)(2,1)S(1)}, u32[]{:S(2)}, u32[]{:S(2)}) collective-permute-start(bf16[32,512]{1,0:T(8,128)(2,1)S(1)} %collective-permute-done.3), channel_id=1, source_target_pairs={{0,1},{1,2},{2,3},{3,4},{4,5},{5,6},{6,7},{7,8},{8,9},{9,10},{10,1... | collective-permute-start | bytes 98312 | tf_op jit(solution)/shard_map/ppermute | solution.py:78
  76.2 7.1 %collective-permute-start.11 = (bf16[32,512]{1,0:T(8,128)(2,1)S(1)}, bf16[32,512]{1,0:T(8,128)(2,1)S(1)}, u32[]{:S(2)}, u32[]{:S(2)}) collective-permute-start(bf16[32,512]{1,0:T(8,128)(2,1)S(1)} %collective-permute-done.10), channel_id=1, source_target_pairs={{1,0},{2,1},{3,2},{4,3},{5,4},{6,5},{7,6},{8,7},{9,8},{10,9},{11,1... | collective-permute-start | bytes 98312 | tf_op jit(solution)/shard_map/ppermute | solution.py:81
  81.4 7.1 %collective-permute-start.5 = (bf16[32,512]{1,0:T(8,128)(2,1)S(1)}, bf16[32,512]{1,0:T(8,128)(2,1)S(1)}, u32[]{:S(2)}, u32[]{:S(2)}) collective-permute-start(bf16[32,512]{1,0:T(8,128)(2,1)S(1)} %collective-permute-done.4), channel_id=1, source_target_pairs={{0,1},{1,2},{2,3},{3,4},{4,5},{5,6},{6,7},{7,8},{8,9},{9,10},{10,1... | collective-permute-start | bytes 98312 | tf_op jit(solution)/shard_map/ppermute | solution.py:78
  83.3 7.1 %collective-permute-start.12 = (bf16[32,512]{1,0:T(8,128)(2,1)S(1)}, bf16[32,512]{1,0:T(8,128)(2,1)S(1)}, u32[]{:S(2)}, u32[]{:S(2)}) collective-permute-start(bf16[32,512]{1,0:T(8,128)(2,1)S(1)} %collective-permute-done.11), channel_id=1, source_target_pairs={{1,0},{2,1},{3,2},{4,3},{5,4},{6,5},{7,6},{8,7},{9,8},{10,9},{11,1... | collective-permute-start | bytes 98312 | tf_op jit(solution)/shard_map/ppermute | solution.py:81
  88.5 7.1 %collective-permute-start.6 = (bf16[32,512]{1,0:T(8,128)(2,1)S(1)}, bf16[32,512]{1,0:T(8,128)(2,1)S(1)}, u32[]{:S(2)}, u32[]{:S(2)}) collective-permute-start(bf16[32,512]{1,0:T(8,128)(2,1)S(1)} %collective-permute-done.5), channel_id=1, source_target_pairs={{0,1},{1,2},{2,3},{3,4},{4,5},{5,6},{6,7},{7,8},{8,9},{9,10},{10,1... | collective-permute-start | bytes 98312 | tf_op jit(solution)/shard_map/ppermute | solution.py:78
  90.4 7.1 %collective-permute-start.13 = (bf16[32,512]{1,0:T(8,128)(2,1)S(1)}, bf16[32,512]{1,0:T(8,128)(2,1)S(1)}, u32[]{:S(2)}, u32[]{:S(2)}) collective-permute-start(bf16[32,512]{1,0:T(8,128)(2,1)S(1)} %collective-permute-done.12), channel_id=1, source_target_pairs={{1,0},{2,1},{3,2},{4,3},{5,4},{6,5},{7,6},{8,7},{9,8},{10,9},{11,1... | collective-permute-start | bytes 98312 | tf_op jit(solution)/shard_map/ppermute | solution.py:81
  95.6 7.1 %collective-permute-start.7 = (bf16[32,512]{1,0:T(8,128)(2,1)S(1)}, bf16[32,512]{1,0:T(8,128)(2,1)S(1)}, u32[]{:S(2)}, u32[]{:S(2)}) collective-permute-start(bf16[32,512]{1,0:T(8,128)(2,1)S(1)} %collective-permute-done.6), channel_id=1, source_target_pairs={{0,1},{1,2},{2,3},{3,4},{4,5},{5,6},{6,7},{7,8},{8,9},{9,10},{10,1... | collective-permute-start | bytes 98312 | tf_op jit(solution)/shard_map/ppermute | solution.py:78
  97.6 6.7 %collective-permute-start.14 = (bf16[32,512]{1,0:T(8,128)(2,1)S(1)}, bf16[32,512]{1,0:T(8,128)(2,1)S(1)}, u32[]{:S(2)}, u32[]{:S(2)}) collective-permute-start(bf16[32,512]{1,0:T(8,128)(2,1)S(1)} %collective-permute-done.13), channel_id=1, source_target_pairs={{1,0},{2,1},{3,2},{4,3},{5,4},{6,5},{7,6},{8,7},{9,8},{10,9},{11,1... | collective-permute-start | bytes 98312 | tf_op jit(solution)/shard_map/ppermute | solution.py:81
  105.6 4.4 %collective-permute-start.15 = (bf16[256,1792]{1,0:T(8,128)(2,1)S(1)}, bf16[256,1792]{1,0:T(8,128)(2,1)S(1)}, u32[]{:S(2)}, u32[]{:S(2)}) collective-permute-start(bf16[256,1792]{1,0:T(8,128)(2,1)S(1)} %convolution_convert_fusion), channel_id=1, source_target_pairs={{0,16},{16,0},{32,48},{48,32},{64,80},{80,64},{96,112},{112,96},{1... | collective-permute-start | bytes 2752520 | tf_op jit(solution)/shard_map/ppermute | solution.py:92
  110.6 19.1 %copy-start.2 = (f32[16,1792]{1,0:T(8,128)S(1)}, f32[16,1792]{1,0:T(8,128)}, u32[]{:S(2)}) copy-start(f32[16,1792]{1,0:T(8,128)} %param.10) | copy-start | bytes 344068
  110.6 19.1 %copy-start.3 = (f32[16,1792]{1,0:T(8,128)S(1)}, f32[16,1792]{1,0:T(8,128)}, u32[]{:S(2)}) copy-start(f32[16,1792]{1,0:T(8,128)} %param.9) | copy-start | bytes 344068
  129.7 21.0 %copy-start.1 = (bf16[512,512]{1,0:T(8,128)(2,1)S(1)}, bf16[512,512]{1,0:T(8,128)(2,1)}, u32[]{:S(2)}) copy-start(bf16[512,512]{1,0:T(8,128)(2,1)} %param.8) | copy-start | bytes 1572868
  148.8 38.3 %collective-permute-start.17 = (bf16[256,1792]{1,0:T(8,128)(2,1)S(1)}, bf16[256,1792]{1,0:T(8,128)(2,1)}, u32[]{:S(2)}, u32[]{:S(2)}) collective-permute-start(bf16[256,1792]{1,0:T(8,128)(2,1)S(1)} %bitcast.55), channel_id=1, source_target_pairs={{0,16},{16,0},{32,48},{48,32},{64,80},{80,64},{96,112},{112,96},{1... | collective-permute-start | bytes 2752520 | tf_op jit(solution)/shard_map/ppermute | solution.py:102
  150.8 35.5 %collective-permute-start.16 = (bf16[256,512]{1,0:T(8,128)(2,1)S(1)}, bf16[256,512]{1,0:T(8,128)(2,1)S(1)}, u32[]{:S(2)}, u32[]{:S(2)}) collective-permute-start(bf16[256,512]{1,0:T(8,128)(2,1)S(1)} %constant_dynamic-slice_fusion), channel_id=1, source_target_pairs={{0,0},{1,47},{2,78},{3,109},{4,140},{5,171},{6,202},{7,233},{8,264... | collective-permute-start | bytes 786440 | tf_op jit(solution)/shard_map/ppermute | solution.py:64
